TPU v7x, 256 devices: a whole 4x4x8 slice. The times are simulated.
256 devices in a mesh: rows: 32 (over z, x_lo, core), cols: 8 (over y, x_hi).
Axes of the slice: x: 4 (x_hi: 2, x_lo: 2; x = x_hi * 2 + x_lo), y: 4, z: 8, core: 2. Of those that a mesh axis runs over, the one named last changes fastest.
Arguments:
- kets: float32 [32, 16, 32], P('rows', 'cols'), may hold values from -3 to 3
- left_maps: float32 [2, 32, 16, 96, 384], P(None, 'rows', 'cols'), may hold values from -0.3125 to 0.3125
- right_maps: float32 [2, 32, 16, 96, 384], P(None, 'rows', 'cols'), may hold values from -0.3125 to 0.3125
- top_edge: float32 [16, 96, 384], P('cols'), may hold values from -6 to 6
- bottom_edge: float32 [16, 96, 384], P('cols'), may hold values from -6 to 6
- left_edge: float32 [32, 96, 384], P('rows'), may hold values from -6 to 6
- right_edge: float32 [32, 96, 384], P('rows'), may hold values from -6 to 6
- term_rows: int32 [16], replicated, may hold values from 0 to 31
- term_bonds: int32 [16], replicated, may hold values from 0 to 14
- term_ops: int32 [16], replicated, may hold values from 0 to 3
- operators: float32 [4, 16], replicated, may hold values from -6 to 6
Outputs:
- top_out: float32 [32, 16, 96, 384], P('rows', 'cols')
- bottom_out: float32 [32, 16, 96, 384], P('rows', 'cols')
- energies: float32 [16], replicated
Inputs may be any that keep to these rules, and one draw needn't show every extreme that they name: Term t acts on the bond between columns term_bonds[t] and term_bonds[t] + 1 of row term_rows[t].
All inputs are finite; a program needn't handle non-finite values.
Results may differ from a plain program's by a relative error of at most 0.0003.
Values sent between devices are 32-bit elements; how exact they have to be, the bound alone decides.
No kernel may reach another device: no remote copies, remote signals or barrier semaphores. Data moves between devices by JAX's collectives and lax.ppermute only.
A program may use at most 64 MiB of HBM per device.

v0:
```python
import functools

import jax
import jax.numpy as jnp
from jax import lax
from jax.experimental import pallas as pl
from jax.experimental.pallas import tpu as pltpu
from jax.sharding import Mesh
from jax.sharding import PartitionSpec as P


D2 = 4
CHI = 96
LANES = 128
EPSILON = 1e-06
F32 = jnp.float32
BF16 = jnp.bfloat16


def split(values):
    high = values.astype(BF16)
    low = (values - high.astype(F32)).astype(BF16)
    return high, low


def split_three(values):
    high = values.astype(BF16)
    rest = values - high.astype(F32)
    middle = rest.astype(BF16)
    low = (rest - middle.astype(F32)).astype(BF16)
    return high, middle, low


def dot(former, latter):
    return lax.dot_general(former, latter, (((1,), (0,)), ((), ())), preferred_element_type=F32)


def dot_t(former, latter):
    return lax.dot_general(former, latter, (((1,), (1,)), ((), ())), preferred_element_type=F32)


def one_hot(rows, cols, test):
    row = lax.broadcasted_iota(jnp.int32, (rows, cols), 0)
    col = lax.broadcasted_iota(jnp.int32, (rows, cols), 1)
    return jnp.where(test(row, col), 1.0, 0.0).astype(BF16)


FINE = ((0, 0), (0, 1), (1, 0), (1, 1), (0, 2), (2, 0))
COARSE = ((0, 0), (0, 1), (1, 0))


def chunks(parts, order, side, axis):
    return jnp.concatenate([parts[pair[side]] for pair in order], axis=axis)


def parts_of(values, order):
    return split_three(values) if order is FINE else split(values)


def join_state(state, rights, turned, order):
    former = chunks(parts_of(state, order), order, 0, 1)
    latter = chunks(rights, order, 1, 1 if turned else 0)
    joined = dot_t(former, latter) if turned else dot(former, latter)
    pieces = []
    for block in range(CHI // 8):
        stacked = [
            joined[block * 32 + i * 8 : block * 32 + i * 8 + 8, j * LANES : (j + 1) * LANES]
            for i in range(D2)
            for j in range(D2)
        ]
        pieces.append(jnp.concatenate(stacked, axis=0))
    mixed = jnp.concatenate(pieces, axis=1)
    return chunks(parts_of(mixed, order), order, 1, 0)


def lane_parts(ref, width, count):
    return [ref[:, part * width : (part + 1) * width] for part in range(count)]


def close_state(joined, mixer, lefts, order):
    mixed = dot(chunks(mixer, order, 0, 1), joined)
    rows = []
    for block in range(CHI // 8):
        for k in range(D2):
            rows.append(
                jnp.concatenate(
                    [
                        mixed[(k * D2 + m) * 8 : (k * D2 + m) * 8 + 8, block * LANES : (block + 1) * LANES]
                        for m in range(D2)
                    ],
                    axis=1,
                )
            )
    through = jnp.concatenate(rows, axis=0)
    renewed = dot(chunks(lefts, order, 0, 1), chunks(parts_of(through, order), order, 1, 0))
    pieces = [
        renewed[block * 8 : block * 8 + 8, m * LANES : (m + 1) * LANES] for block in range(CHI // 8) for m in range(D2)
    ]
    return jnp.concatenate(pieces, axis=0)


def expand_mixer(site):
    spread = one_hot(LANES, 16, lambda r, c: (r >> 3) == c)
    gather = one_hot(16, LANES, lambda r, c: (c >> 3) == r)
    row = lax.broadcasted_iota(jnp.int32, (LANES, LANES), 0)
    col = lax.broadcasted_iota(jnp.int32, (LANES, LANES), 1)
    same = (row & 7) == (col & 7)
    parts = []
    for part in split_three(site):
        wide = dot(spread, dot(part, gather).astype(BF16))
        parts.append(jnp.where(same, wide, 0.0).astype(BF16))
    return jnp.concatenate(parts, axis=1)


LEFT_ROW = D2 * LANES
MIXER_ROW = LEFT_ROW + 3 * CHI
PACKED = MIXER_ROW + LANES


def prep_body(own_ref, other_ref, maps_ref, *rest):
    deal_ref, dense_ref = rest[-2:]

    @pl.when(pl.program_id(0) == 0)
    def _():
        deal_ref[...] = one_hot(
            4 * CHI, D2 * LANES, lambda r, c: (r == (c & 127) * 4 + (c >> 7)) & ((c & 127) < CHI)
        )
        dense_ref[...] = one_hot(
            4 * CHI, 4 * CHI, lambda r, c: (r & 3 == (c >> 3) & 3) & (r >> 2 == (c >> 5) * 8 + (c & 7))
        )

    deal = deal_ref[...]
    dense = dense_ref[...]
    blank = jnp.zeros((LANES - CHI, 3 * LANES), BF16)
    refs = (other_ref, own_ref)
    parts = [part for ref in refs for part in split_three(ref[0, 0:CHI, :])]
    lefts = dot(jnp.concatenate(parts, axis=0), dense).astype(BF16)
    parts = [part for ref in refs for part in split_three(ref[0, CHI : 2 * CHI, :])]
    rights = dot(jnp.concatenate(parts, axis=0), deal).astype(BF16)
    for parity, ref in enumerate(refs):
        maps_ref[parity, LEFT_ROW:MIXER_ROW, :] = lefts[parity * 3 * CHI : (parity + 1) * 3 * CHI]
        for j in range(D2):
            starts = [(parity * 3 + part) * CHI for part in range(3)]
            maps_ref[parity, j * LANES : j * LANES + CHI, :] = jnp.concatenate(
                [rights[start : start + CHI, j * LANES : (j + 1) * LANES] for start in starts], axis=1
            )
            maps_ref[parity, j * LANES + CHI : (j + 1) * LANES, :] = blank
        maps_ref[parity, MIXER_ROW:PACKED, :] = expand_mixer(ref[0, 2 * CHI :, 0:16])


def prep_maps(own, other):
    block = pl.BlockSpec((1, 2 * CHI + 16, 4 * CHI), lambda t: (t, 0, 0))
    unwritten = jax.ShapeDtypeStruct((4, CHI, 4 * CHI), F32)
    return pl.pallas_call(
        prep_body,
        grid=(4,),
        in_specs=[block, block],
        out_specs=[pl.BlockSpec((2, PACKED, 4 * CHI), lambda t: (t, 0, 0))] + [pl.BlockSpec(memory_space=pl.ANY)] * 5,
        out_shape=[jax.ShapeDtypeStruct((8, PACKED, 4 * CHI), BF16)]
        + [unwritten] * 4
        + [jax.ShapeDtypeStruct((CHI, 4 * CHI), F32)],
        scratch_shapes=[pltpu.VMEM((4 * CHI, D2 * LANES), BF16), pltpu.VMEM((4 * CHI, 4 * CHI), BF16)],
        name="prep_maps",
    )(own, other)


def load_state(state_ref, flat):
    for block in range(CHI // 8):
        for i in range(D2):
            start = block * 32 + i * 8
            state_ref[start : start + 8, 0:CHI] = flat[block * 8 : block * 8 + 8, i * CHI : (i + 1) * CHI]


def store_state(store, state, scale):
    for i in range(D2):
        pieces = [state[block * 32 + i * 8 : block * 32 + i * 8 + 8, 0:CHI] for block in range(CHI // 8)]
        store(slice(i * CHI, (i + 1) * CHI), jnp.concatenate(pieces, axis=0) * scale)


def inverse_norm(state):
    total = jnp.sum(jnp.sum(state * state, axis=0, keepdims=True), axis=1, keepdims=True)
    return 1.0 / jnp.sqrt(total * (1.0 / (4 * CHI * CHI)) + EPSILON)


def chain_body(
    upward,
    start_ref,
    maps_ref,
    fed_even,
    fed_odd,
    made_even,
    made_odd,
    last_ref,
    state_ref,
    slots_ref,
    flats_ref,
    slot_sems,
    fed_sems,
    made_sems,
):
    def row_of(step):
        return jnp.where(upward[0] == 1, 7 - step, step)

    def fetch(step, slot):
        return pltpu.make_async_copy(maps_ref.at[row_of(step)], slots_ref.at[slot], slot_sems.at[slot])

    def send(target, step, row, sems):
        return pltpu.make_async_copy(flats_ref.at[step], target.at[row >> 1], sems.at[row])

    fetch(0, 0).start()
    state_ref[...] = jnp.zeros_like(state_ref)
    load_state(state_ref, start_ref[...])

    def scaled_state(step):
        state = state_ref[...]
        scale = jnp.where(step == 0, 1.0, inverse_norm(state))

        def store(lanes, value):
            flats_ref[step, :, lanes] = value

        store_state(store, state, scale)
        return state, scale

    def send_rows(even, odd, step, row, sems):
        @pl.when(row & 1 == 0)
        def _():
            send(even, step, row, sems).start()

        @pl.when(row & 1 == 1)
        def _():
            send(odd, step, row, sems).start()

    def one_row(step, carry):
        slot = step & 1

        @pl.when(step < 7)
        def _():
            fetch(step + 1, 1 - slot).start()

        fetch(step, slot).wait()
        state, scale = scaled_state(step)
        maps = slots_ref.at[slot]
        rights = [maps[0:LEFT_ROW, part * LANES : (part + 1) * LANES] for part in range(3)]
        left = [maps[LEFT_ROW + part * CHI : LEFT_ROW + (part + 1) * CHI, :] for part in range(3)]
        mixer = [maps[MIXER_ROW:PACKED, part * LANES : (part + 1) * LANES] for part in range(3)]
        state_ref[...] = close_state(join_state(state, rights, True, FINE), mixer, left, FINE) * scale
        send_rows(fed_even, fed_odd, step, row_of(step), fed_sems)

        @pl.when(step > 0)
        def _():
            send_rows(made_even, made_odd, step, row_of(step - 1), made_sems)

        return carry

    lax.fori_loop(0, 8, one_row, 0)
    scaled_state(8)
    last_ref[...] = flats_ref[8]
    send_rows(made_even, made_odd, 8, row_of(7), made_sems)
    for row in range(8):
        send(fed_odd if row & 1 else fed_even, 0, row, fed_sems).wait()
        send(made_odd if row & 1 else made_even, 0, row, made_sems).wait()


def run_chain(upward, start, maps):
    flat_spec = pl.BlockSpec((CHI, 4 * CHI), lambda step, up: (0, 0))
    anywhere = pl.BlockSpec(memory_space=pl.ANY)
    grid_spec = pltpu.PrefetchScalarGridSpec(
        num_scalar_prefetch=1,
        grid=(1,),
        in_specs=[flat_spec, anywhere],
        out_specs=[anywhere, anywhere, anywhere, anywhere, flat_spec],
        scratch_shapes=[
            pltpu.VMEM((4 * CHI, LANES), F32),
            pltpu.VMEM((2, PACKED, 4 * CHI), BF16),
            pltpu.VMEM((9, CHI, 4 * CHI), F32),
            pltpu.SemaphoreType.DMA((2,)),
            pltpu.SemaphoreType.DMA((8,)),
            pltpu.SemaphoreType.DMA((8,)),
        ],
    )
    rows = jax.ShapeDtypeStruct((4, CHI, 4 * CHI), F32)
    return pl.pallas_call(
        chain_body,
        grid_spec=grid_spec,
        out_shape=[rows, rows, rows, rows, jax.ShapeDtypeStruct((CHI, 4 * CHI), F32)],
        name="run_chain",
    )(upward, start, maps)


def mix_sites_body(sites_ref, mixers_ref, opens_ref, rho_ref):
    for kind in range(2):
        for index in range(5):
            mixers_ref[kind, 0, index] = expand_mixer(sites_ref[kind, 0, index])[:, : 2 * LANES]


def mix_sites(sites):
    return pl.pallas_call(
        mix_sites_body,
        grid=(5,),
        in_specs=[pl.BlockSpec((2, 1, 5, 16, 16), lambda t: (0, t, 0, 0, 0))],
        out_specs=[
            pl.BlockSpec((2, 1, 5, LANES, 2 * LANES), lambda t: (0, t, 0, 0, 0)),
            pl.BlockSpec(memory_space=pl.ANY),
            pl.BlockSpec(memory_space=pl.ANY),
        ],
        out_shape=[
            jax.ShapeDtypeStruct((2, 5, 5, LANES, 2 * LANES), BF16),
            jax.ShapeDtypeStruct((4, 4, 4 * CHI, LANES), F32),
            jax.ShapeDtypeStruct((5, 8, LANES), F32),
        ],
        name="mix_sites",
    )(sites)


def prep_lefts_body(cols_ref, beside_ref, lefts_ref, blank_ref, work_ref, deal_ref, put_ref):
    @pl.when(pl.program_id(0) == 0)
    def _():
        work_ref[...] = jnp.zeros_like(work_ref)
        deal_ref[...] = one_hot(4 * CHI, 4 * CHI, lambda r, c: r == ((c >> 3) & 3) * CHI + (c >> 5) * 8 + (c & 7))
        put_ref[...] = one_hot(D2 * LANES, 4 * CHI, lambda r, c: r == ((c >> 3) & 3) * LANES + (c >> 5) * 8 + (c & 7))

    deal = deal_ref[...]
    put = put_ref[...]
    col = jnp.where(pl.program_id(0) == 4, beside_ref[...], cols_ref[0])
    lefts_ref[1, 0] = side_by_side(dot(jnp.concatenate(split(col), axis=0), deal).astype(BF16))
    for i in range(D2):
        work_ref[0:CHI, i * LANES : i * LANES + CHI] = col[:, i * CHI : (i + 1) * CHI]
    turned = [jnp.transpose(work_ref[:, i * LANES : (i + 1) * LANES])[0:CHI] for i in range(D2)]
    parts = split(jnp.concatenate(turned, axis=1))
    lefts_ref[0, 0] = side_by_side(dot(jnp.concatenate(parts, axis=0), put).astype(BF16))


def side_by_side(stacked):
    return jnp.concatenate([stacked[0:CHI], stacked[CHI:]], axis=1)


def prep_lefts(cols, beside):
    return pl.pallas_call(
        prep_lefts_body,
        grid=(5,),
        in_specs=[
            pl.BlockSpec((1, CHI, 4 * CHI), lambda t: (jnp.minimum(t, 3), 0, 0)),
            pl.BlockSpec((CHI, 4 * CHI), lambda t: (0, 0)),
        ],
        out_specs=[
            pl.BlockSpec((2, 1, CHI, 8 * CHI), lambda t: (0, t, 0, 0)),
            pl.BlockSpec(memory_space=pl.ANY),
        ],
        out_shape=[
            jax.ShapeDtypeStruct((2, 5, CHI, 8 * CHI), BF16),
            jax.ShapeDtypeStruct((CHI, 4 * CHI), F32),
        ],
        scratch_shapes=[
            pltpu.VMEM((LANES, D2 * LANES), F32),
            pltpu.VMEM((4 * CHI, 4 * CHI), BF16),
            pltpu.VMEM((D2 * LANES, 4 * CHI), BF16),
        ],
        name="prep_lefts",
    )(cols, beside)


def walk_body(second, control, start_ref, cols_ref, beside_ref, lefts_ref, mixers_ref, *refs):
    if second:
        given_ref, rho_ref, last_ref, *scratch = refs
    else:
        _, given_ref, last_ref, *scratch = refs
    state_ref, work_ref, joined_ref, col_buf, left_buf, closed_buf, mixer_buf, open_buf, sems = scratch
    kind = control[0]

    def bond_of(step):
        return jnp.where(kind == 0, step, 3 - step)

    def needed(step):
        return control[2 + bond_of(step)] == 1

    def col_copy(source, step):
        return pltpu.make_async_copy(source, col_buf.at[step], sems.at[step, 0])

    def map_copies(step):
        col = bond_of(step) + kind
        return [
            pltpu.make_async_copy(lefts_ref.at[kind, col], left_buf.at[step], sems.at[step, 1]),
            pltpu.make_async_copy(mixers_ref.at[kind, col, 4], closed_buf.at[step], sems.at[step, 2]),
        ]

    def open_copies(step):
        col = bond_of(step) + kind
        copies = [pltpu.make_async_copy(mixers_ref.at[kind, col, pl.ds(0, 4)], mixer_buf.at[step], sems.at[step, 3])]
        if second:
            copies.append(pltpu.make_async_copy(given_ref.at[bond_of(step)], open_buf.at[step], sems.at[step, 4]))
        return copies

    def keep_copy(step):
        return pltpu.make_async_copy(open_buf.at[step], given_ref.at[bond_of(step)], sems.at[step, 4])

    for step in range(4):
        col = bond_of(step) + kind

        @pl.when(col == 4)
        def _():
            col_copy(beside_ref, step).start()

        @pl.when(col < 4)
        def _():
            col_copy(cols_ref.at[jnp.minimum(col, 3)], step).start()

        for copy in map_copies(step):
            copy.start()

        @pl.when(needed(step))
        def _():
            for copy in open_copies(step):
                copy.start()

    state_ref[...] = jnp.zeros_like(state_ref)
    work_ref[...] = jnp.zeros_like(work_ref)
    load_state(state_ref, start_ref[...])
    if second:
        rho_ref[...] = jnp.zeros_like(rho_ref)

    def one_column(step, fresh):
        col_copy(beside_ref, step).wait()
        for copy in map_copies(step):
            copy.wait()

        @pl.when(needed(step))
        def _():
            for copy in open_copies(step):
                copy.wait()

        state = state_ref[...]
        scale = jnp.where(fresh == 1, 1.0, inverse_norm(state))
        passed = (step == 0) & (control[1] == 1)
        left = lane_parts(left_buf.at[step], 4 * CHI, 2)

        @pl.when(jnp.logical_not(passed))
        def _():
            for j in range(D2):
                work_ref[:, j * LANES : j * LANES + CHI] = col_buf[step, :, j * CHI : (j + 1) * CHI]
            parts = split(work_ref[...])

            @pl.when(kind == 0)
            def _():
                pad = jnp.zeros((LANES - CHI, D2 * LANES), BF16)
                rights = [jnp.concatenate([part, pad], axis=0) for part in parts]
                joined_ref[...] = join_state(state, rights, False, COARSE)

            @pl.when(kind == 1)
            def _():
                pad = jnp.zeros((LANES - CHI, LANES), BF16)
                rights = []
                for part in parts:
                    rows = []
                    for j in range(D2):
                        rows += [part[:, j * LANES : (j + 1) * LANES], pad]
                    rights.append(jnp.concatenate(rows, axis=0))
                joined_ref[...] = join_state(state, rights, True, COARSE)

        @pl.when(jnp.logical_not(passed | needed(step)))
        def _():
            mixer = lane_parts(closed_buf.at[step], LANES, 2)
            state_ref[...] = close_state(joined_ref[...], mixer, left, COARSE) * scale

        @pl.when(needed(step) & jnp.logical_not(passed))
        def _():
            lane = lax.broadcasted_iota(jnp.int32, (8, LANES), 1)
            state_ref[...] = jnp.zeros_like(state_ref)

            def one_open(index, found):
                mixer = lane_parts(mixer_buf.at[step, index], LANES, 2)
                opened = close_state(joined_ref[...], mixer, left, COARSE) * scale
                state_ref[...] += opened * jnp.where((index == 0) | (index == 3), 1.0, 0.0)
                if second:
                    for other in range(4):
                        total = jnp.sum(opened * open_buf[step, other], axis=0, keepdims=True)
                        value = jnp.sum(total, axis=1, keepdims=True)
                        spot = jnp.where(kind == 0, index * 4 + other, other * 4 + index)
                        found = found + jnp.where(lane == spot, value, 0.0)
                else:
                    open_buf[step, index] = opened
                return found

            found = lax.fori_loop(0, 4, one_open, jnp.zeros((8, LANES), F32))
            if second:
                rho_ref[bond_of(step)] = found
            else:
                keep_copy(step).start()

        return jnp.where(passed, fresh, 0)

    lax.fori_loop(0, 4, one_column, jnp.int32(1))
    state = state_ref[...]

    def store(lanes, value):
        last_ref[:, lanes] = value

    store_state(store, state, inverse_norm(state))
    if not second:
        for step in range(4):

            @pl.when(needed(step))
            def _():
                keep_copy(step).wait()


def run_walk(second, control, start, cols, beside, lefts, mixers, opens):
    flat_spec = pl.BlockSpec((CHI, 4 * CHI), lambda step, control: (0, 0))
    anywhere = pl.BlockSpec(memory_space=pl.ANY)
    flat = jax.ShapeDtypeStruct((CHI, 4 * CHI), F32)
    if second:
        out_specs = [pl.BlockSpec((5, 8, LANES), lambda step, control: (0, 0, 0)), flat_spec]
        out_shape = [jax.ShapeDtypeStruct((5, 8, LANES), F32), flat]
    else:
        out_specs = [anywhere, flat_spec]
        out_shape = [jax.ShapeDtypeStruct((4, 4, 4 * CHI, LANES), F32), flat]
    grid_spec = pltpu.PrefetchScalarGridSpec(
        num_scalar_prefetch=1,
        grid=(1,),
        in_specs=[flat_spec] + [anywhere] * 5,
        out_specs=out_specs,
        scratch_shapes=[
            pltpu.VMEM((4 * CHI, LANES), F32),
            pltpu.VMEM((CHI, D2 * LANES), F32),
            pltpu.VMEM((3 * LANES, CHI // 8 * LANES), BF16),
            pltpu.VMEM((4, CHI, 4 * CHI), F32),
            pltpu.VMEM((4, CHI, 8 * CHI), BF16),
            pltpu.VMEM((4, LANES, 2 * LANES), BF16),
            pltpu.VMEM((4, 4, LANES, 2 * LANES), BF16),
            pltpu.VMEM((4, 4, 4 * CHI, LANES), F32),
            pltpu.SemaphoreType.DMA((4, 5)),
        ],
    )
    return pl.pallas_call(
        functools.partial(walk_body, second),
        grid_spec=grid_spec,
        out_shape=out_shape,
        input_output_aliases={} if second else {6: 0},
        name="second_walk" if second else "first_walk",
    )(control, start, cols, beside, lefts, mixers, opens)


def finish_body(place, term_rows, term_bonds, term_ops, rho_ref, operators_ref, share_ref, total_ref):
    lane = lax.broadcasted_iota(jnp.int32, (1, TERMS), 1)
    diagonal = ((lane == 0) | (lane == 3) | (lane == 12) | (lane == 15)).astype(F32)
    total_ref[...] = jnp.zeros_like(total_ref)
    for term in range(TERMS):
        bond = term_bonds[term] - 4 * place[1]

        @pl.when((term_rows[term] == place[0]) & (bond >= 0) & (bond < 4) & (place[2] == 1))
        def _():
            density = rho_ref[jnp.clip(bond, 0, 3), 0:1, 0:TERMS]
            trace = jnp.sum(density * diagonal, axis=1, keepdims=True)
            spread = jnp.sqrt(jnp.sum(density * density, axis=1, keepdims=True))
            weights = operators_ref[pl.ds(term_ops[term], 1), :]
            value = jnp.sum(density * weights, axis=1, keepdims=True) / jnp.maximum(jnp.abs(trace), 0.25 * spread)
            total_ref[...] = total_ref[...] + jnp.where(lane == term, value, 0.0)

    share_ref[...] = jnp.broadcast_to(total_ref[...], share_ref.shape)


def finish_terms(place, term_rows, term_bonds, term_ops, rho, operators):
    grid_spec = pltpu.PrefetchScalarGridSpec(
        num_scalar_prefetch=4,
        grid=(1,),
        in_specs=[
            pl.BlockSpec((5, 8, LANES), lambda step, *_: (0, 0, 0)),
            pl.BlockSpec((OPS, TERMS), lambda step, *_: (0, 0)),
        ],
        out_specs=[pl.BlockSpec((256, TERMS), lambda step, *_: (0, 0))],
        scratch_shapes=[pltpu.VMEM((1, TERMS), F32)],
    )
    return pl.pallas_call(
        finish_body,
        grid_spec=grid_spec,
        out_shape=[jax.ShapeDtypeStruct((256, TERMS), F32)],
        name="finish_terms",
    )(place, term_rows, term_bonds, term_ops, rho, operators)[0]


BLOCK = ("b", "zz", "xl", "co", "y", "xh")
ROWS = ("b", "zz", "xl", "co")
COLS = ("y", "xh")
TERMS = 16
OPS = 4


def open_sites(kets):
    ket = kets.reshape(kets.shape[0], 2, 1, 2, 1, 2, 1, 2, 1, 2, 1)
    bra = kets.reshape(kets.shape[0], 1, 2, 1, 2, 1, 2, 1, 2, 1, 2)
    return (ket * bra).reshape(-1, 4, D2, D2, D2, D2)


def core_shared(even, odd, core):
    return jnp.where(core == 1, odd, lax.ppermute(even, "co", [(1, 0)]))


def shards(
    kets,
    left_maps,
    right_maps,
    top_edge,
    bottom_edge,
    left_edge,
    right_edge,
    term_rows,
    term_bonds,
    term_ops,
    operators,
):
    b, zz, xl, core, y, xh = (lax.axis_index(name) for name in BLOCK)
    high = b >= 2
    upward = zz
    stage = jnp.where(upward == 0, b, 3 - b)
    late = jnp.where(high, zz == 0, zz == 1)

    opened = open_sites(kets[0])
    closed = opened[:, 0] + opened[:, 3]
    down_site = jnp.transpose(closed, (0, 2, 3, 1, 4)).reshape(2, 16, 16)
    up_site = jnp.transpose(closed, (0, 2, 1, 3, 4)).reshape(2, 16, 16)
    sites = jnp.stack([down_site, up_site])
    extra = jnp.concatenate(
        [
            jnp.pad(sites, ((0, 0), (0, 0), (0, 0), (0, LANES - 16))),
            jnp.pad(jnp.broadcast_to(opened.reshape(1, 2, 16, 64), (2, 2, 16, 64)), ((0, 0), (0, 0), (0, 0), (0, 64))),
        ],
        axis=3,
    )
    extra = jnp.pad(extra, ((0, 0), (0, 0), (0, 0), (0, LANES)))
    payload = jnp.concatenate([left_maps[:, 0], right_maps[:, 0], extra], axis=2)
    own = lax.all_to_all(payload.reshape(4, 2 * CHI + 16, 4 * CHI), ("zz", "xl"), 0, 0)
    other = lax.ppermute(own, "co", [(0, 1)])
    maps, *rows, unused = prep_maps(own, other)

    start = jnp.where(
        upward == 0,
        lax.dynamic_index_in_dim(top_edge, xl, 0, keepdims=False),
        lax.dynamic_index_in_dim(bottom_edge, xl, 0, keepdims=False),
    )
    direction = upward.reshape(1).astype(jnp.int32)
    source = start
    hops = [[((k, 0), (k + 1, 0)), ((3 - k, 1), (2 - k, 1))] for k in range(3)]

    def run_stage(k, source, rows):
        *rows, last = lax.cond(
            (stage == k) & (core == 1),
            lambda source, unused, *rows: tuple(run_chain(direction, source, maps)),
            lambda source, unused, *rows: rows + (unused,),
            source,
            unused,
            *rows,
        )
        return rows, last

    def hop(k, last):
        pairs = [((p * 2 + q) * 2 + 1, (r * 2 + s) * 2 + 1) for (p, q), (r, s) in hops[k]]
        return lax.ppermute(last, ("b", "zz", "co"), pairs)

    rows, last = run_stage(0, source, rows)
    source = hop(0, last)

    carried = own[:, 2 * CHI :, LANES : LANES + 64].reshape(4, 8, LANES)
    carried = lax.all_to_all(carried, ("xh", "xl"), 0, 0)
    carried_beside = lax.ppermute(carried[0], "y", [(1, 0), (2, 1), (3, 2)])
    tensors = jnp.concatenate([carried, carried_beside[None]], axis=0).reshape(5, 4, D2, D2, D2, D2)
    tensors = jnp.concatenate([tensors, (tensors[:, 0] + tensors[:, 3])[:, None]], axis=1)
    tensors = jnp.where(high, jnp.transpose(tensors, (0, 1, 4, 3, 2, 5)), tensors)
    walk_sites = jnp.stack(
        [
            jnp.transpose(tensors, (0, 1, 2, 5, 3, 4)).reshape(5, 5, 16, 16),
            jnp.transpose(tensors, (0, 1, 2, 3, 5, 4)).reshape(5, 5, 16, 16),
        ]
    )
    walk_mixers, opens, rho = mix_sites(walk_sites)
    edge = jnp.where(y < 2, left_edge[0], right_edge[0])
    moved_edge = lax.ppermute(edge, ("b", "zz", "xh"), [(0, 2), (4, 6), (11, 9), (15, 13)])
    edge = jnp.where((xh == 1) == (zz == 1), edge, moved_edge)
    turned_edge = jnp.transpose(edge.reshape(CHI, D2, CHI), (2, 1, 0)).reshape(CHI, D2 * CHI)
    edge = lax.optimization_barrier(jnp.where(high, turned_edge, edge))

    rows, last = run_stage(1, source, rows)
    source = hop(1, last)

    early = core_shared(rows[0], rows[1], core)
    early = lax.all_to_all(early, ("xh", "xl"), 0, 0)
    source, early = lax.optimization_barrier((source, early))
    early = lax.ppermute(early, ("b", "zz"), [(0, 1), (2, 3), (5, 4), (7, 6)])

    rows, last = run_stage(2, source, rows)
    source = hop(2, last)
    rows, last = run_stage(3, source, rows)

    lates = core_shared(rows[0], rows[1], core)
    lates = lax.all_to_all(lates, ("xh", "xl"), 0, 0)
    early, _ = lax.optimization_barrier((early, last))
    early_beside = lax.ppermute(early[0], "y", [(1, 0), (2, 1), (3, 2)])
    walk_lefts, blank = prep_lefts(early, early_beside)
    beside = lax.ppermute(lates[0], "y", [(1, 0), (2, 1), (3, 2)])

    row = 8 * b + 4 * xh + 2 * xl + core
    bonds = 4 * y + jnp.arange(4, dtype=jnp.int32)
    matched = (term_rows[:, None] == row) & (term_bonds[:, None] == bonds[None, :]) & late
    needs = jnp.any(matched, axis=0)
    kind = jnp.where(y < 2, 0, 1)
    passes = jnp.where(y == 3, 1, 0)
    first_control = jnp.concatenate([jnp.stack([kind, passes]), needs.astype(jnp.int32)]).astype(jnp.int32)
    second_control = jnp.concatenate([jnp.stack([1 - kind, 0 * passes]), needs.astype(jnp.int32)]).astype(jnp.int32)
    env = edge

    def first_step(active, env, opens, beside):
        return lax.cond(
            active,
            lambda env, unused, opens: tuple(
                run_walk(False, first_control, env, lates, beside, walk_lefts, walk_mixers, opens)
            ),
            lambda env, unused, opens: (opens, unused),
            env,
            unused,
            opens,
        )

    def second_step(active, env, rho):
        return lax.cond(
            active,
            lambda env, unused, rho: tuple(
                run_walk(True, second_control, env, lates, beside, walk_lefts, walk_mixers, opens)
            ),
            lambda env, unused, rho: (rho, unused),
            env,
            unused,
            rho,
        )

    def env_hop(pairs, env):
        lates = (1, 3, 4, 6)
        return lax.ppermute(env, ("b", "zz", "y"), [(4 * place + p, 4 * place + q) for place in lates for p, q in pairs])

    outer = late & ((y == 0) | (y == 3))
    inner = late & ((y == 1) | (y == 2))
    opens, env = first_step(outer, env, opens, blank)
    rows, env = lax.optimization_barrier((rows, env))
    env = env_hop([(0, 1), (3, 2)], env)

    placed = lax.all_to_all(core_shared(rows[2], rows[3], core), ("zz", "xl"), 0, 0).reshape(2, 2, CHI, 4 * CHI)

    opens, env = first_step(inner, env, opens, beside)
    env = env_hop([(1, 2), (2, 1)], env)
    rho, env = second_step(inner, env, rho)
    env = env_hop([(2, 3), (1, 0)], env)
    rho, env = second_step(outer, env, rho)

    place = jnp.stack([row, y, late.astype(jnp.int32)]).astype(jnp.int32)
    shares = finish_terms(place, term_rows, term_bonds, term_ops, rho, operators)
    energies = jnp.sum(lax.all_to_all(shares, BLOCK, 0, 0), axis=0)
    top_out, bottom_out = placed[0][None], placed[1][None]
    return top_out, bottom_out, energies


def solution(mesh):
    torus = Mesh(mesh.devices.reshape(4, 2, 2, 2, 4, 2), BLOCK)
    placed = (
        P(ROWS, COLS, None),
        P(None, ROWS, COLS, None, None),
        P(None, ROWS, COLS, None, None),
        P(COLS, None, None),
        P(COLS, None, None),
        P(ROWS, None, None),
        P(ROWS, None, None),
        P(),
        P(),
        P(),
        P(),
    )

    return jax.shard_map(
        shards,
        mesh=torus,
        in_specs=placed,
        out_specs=(P(ROWS, COLS, None, None), P(ROWS, COLS, None, None), P()),
        check_vma=False,
    )
```

profile of v0, /device:TPU:8, one launch (start us, length us, event | category | flops | bytes accessed | tf_op | source)
XLA Modules:
  0.0 259.5 jit_solution(12900703213648762020)
XLA Ops:
  0.6 0.8 mul.35
  1.4 0.2 broadcast_multiply_fusion
  1.6 0.7 mul.40
  2.3 0.4 reshape.70
  3.1 20.6 %all_to_all.34.own_ref = f32[4,208,384]{2,1,0:T(8,128)S(1)} all-to-all(f32[4,208,384]{2,1,0:T(8,128)S(1)} %pad_maximum_fusion), channel_id=1, replica_groups=mesh['b'=4,'zz'=2,'xl'=2,'co'=2,'y'=4,'xh'=2] {'zz','xl'}, dimensions={0} | all-to-all | bytes 2555904 | tf_op jit(solution)/shard_map/all_to_all | solution.py:630
  23.7 2.6 collective-permute-start
  26.3 1.6 collective-permute-done.other_ref
  27.9 8.4 %prep_maps.1 = (bf16[8,928,384]{2,1,0:T(8,128)(2,1)}, f32[4,96,384]{2,1,0:T(8,128)S(1)}, f32[4,96,384]{2,1,0:T(8,128)S(1)}, f32[4,96,384]{2,1,0:T(8,128)}, f32[4,96,384]{2,1,0:T(8,128)}, /*index=5*/f32[96,384]{1,0:T(8,128)S(1)}) custom-call(f32[4,208,384]{2,1,0:T(8,128)} %copy-done, f32[4,208,384]{2,1,0:T(8,128)} %collective-permute-done.other_ref), custom_call_target="tpu_custom_call" | custom-call | tf_op jit(solution)/shard_map/prep_maps/pallas_call | solution.py:154
  36.3 0.7 collective-permute-start.1
  37.1 1.4 collective-permute-start.3
  38.6 2.7 %collective-permute-start.6 = (f32[96,384]{1,0:T(8,128)S(1)}, f32[96,384]{1,0:T(8,128)S(1)}, u32[]{:S(2)}, u32[]{:S(2)}) collective-permute-start(f32[96,384]{1,0:T(8,128)S(1)} %select_bitcast_fusion.1), channel_id=1, source_target_pairs={{0,32},{64,96},{161,129},{225,193},{2,34},{66,98},{163,131},{227,1... | collective-permute-start | bytes 442376 | tf_op jit(solution)/shard_map/ppermute | solution.py:675
  41.4 18.1 %collective-permute-done.3 = f32[4,96,384]{2,1,0:T(8,128)S(1)} collective-permute-done((f32[4,96,384]{2,1,0:T(8,128)S(1)}, f32[4,96,384]{2,1,0:T(8,128)S(1)}, u32[]{:S(2)}, u32[]{:S(2)}) %collective-permute-start.3) | collective-permute-done | bytes 589856 | tf_op jit(solution)/shard_map/ppermute | solution.py:594
  59.4 0.9 broadcast_select_fusion.2
  60.3 4.1 %all-to-all-start.1 = ((f32[4,96,384]{2,1,0:T(8,128)}), f32[4,96,384]{2,1,0:T(8,128)}, u32[]{:S(2)}, u32[]{:S(2)}) async-start(f32[4,96,384]{2,1,0:T(8,128)} %broadcast_select_fusion.2), calls=%async_computation.1 | async-start | bytes 1179648 | tf_op jit(solution)/shard_map/all_to_all | solution.py:684
  64.5 0.2 and_reduce_fusion
  64.8 0.2 reshape.67
  65.1 0.1 reshape.68
  65.3 0.8 slice.50
  66.0 0.7 reshape.66
  66.7 0.7 collective-permute-start.2
  67.4 7.9 %all-to-all-done.1 = f32[4,96,384]{2,1,0:T(8,128)} async-done(((f32[4,96,384]{2,1,0:T(8,128)}), f32[4,96,384]{2,1,0:T(8,128)}, u32[]{:S(2)}, u32[]{:S(2)}) %all-to-all-start.1) | async-done | bytes 589856 | tf_op jit(solution)/shard_map/all_to_all | solution.py:684
  75.3 3.3 %all-to-all-start.2 = ((f32[4,8,128]{2,1,0:T(8,128)}), f32[4,8,128]{2,1,0:T(8,128)S(1)}, u32[]{:S(2)}, u32[]{:S(2)}) async-start(f32[4,8,128]{2,1,0:T(8,128)} %reshape.66), calls=%async_computation.2 | async-start | bytes 32768 | tf_op jit(solution)/shard_map/all_to_all | solution.py:662
  78.6 0.7 broadcast_select_fusion.4
  79.3 0.7 collective-permute-start.4
  79.9 3.9 %all-to-all-done.2 = f32[4,8,128]{2,1,0:T(8,128)S(1)} async-done(((f32[4,8,128]{2,1,0:T(8,128)}), f32[4,8,128]{2,1,0:T(8,128)S(1)}, u32[]{:S(2)}, u32[]{:S(2)}) %all-to-all-start.2) | async-done | bytes 16416 | tf_op jit(solution)/shard_map/all_to_all | solution.py:662
  83.9 2.3 collective-permute-start.5
  86.2 0.7 concatenate.35
  86.9 1.3 collective-permute-start.8
  88.3 1.3 collective-permute-start.7
  89.6 0.2 concatenate.36
  89.9 0.3 pad_maximum_fusion.1
  90.2 9.2 %collective-permute-done.8.cols_ref = f32[4,96,384]{2,1,0:T(8,128)S(1)} collective-permute-done((f32[4,96,384]{2,1,0:T(8,128)}, f32[4,96,384]{2,1,0:T(8,128)S(1)}, u32[]{:S(2)}, u32[]{:S(2)}) %collective-permute-start.8) | collective-permute-done | bytes 589856 | tf_op jit(solution)/shard_map/ppermute | solution.py:686
  99.4 1.0 broadcast_select_fusion.1
  100.4 4.2 %all-to-all-start.3 = ((f32[4,96,384]{2,1,0:T(8,128)}), f32[4,96,384]{2,1,0:T(8,128)}, u32[]{:S(2)}, u32[]{:S(2)}) async-start(f32[4,96,384]{2,1,0:T(8,128)} %broadcast_select_fusion.1), calls=%async_computation.3 | async-start | bytes 1179648 | tf_op jit(solution)/shard_map/all_to_all | solution.py:693
  104.6 0.7 slice_bitcast_fusion.3
  105.2 2.1 collective-permute-start.9
  107.3 0.6 fusion.1
  108.0 2.7 %copy.40 = f32[5,5,4,4,4,4]{5,4,3,2,1,0:T(4,128)S(1)} copy(f32[5,5,4,4,4,4]{4,5,3,2,1,0:T(4,128)S(1)} %get-tuple-element.342) | data formatting | bytes 51200 | tf_op jit(solution)/shard_map/transpose | solution.py:670
  110.7 0.4 stack_reshape.15
  111.1 2.7 %copy.39 = f32[5,5,4,4,4,4]{5,4,3,2,1,0:T(4,128)S(1)} copy(f32[5,5,4,4,4,4]{3,5,4,2,1,0:T(4,128)S(1)} %get-tuple-element.341) | data formatting | bytes 51200 | tf_op jit(solution)/shard_map/transpose | solution.py:669
  113.8 0.4 stack_reshape.14
  114.2 0.8 pad_maximum_fusion.2.sites_ref
  115.0 8.9 %mix_sites.1 = (bf16[2,5,5,128,256]{4,3,2,1,0:T(8,128)(2,1)S(1)}, f32[4,4,384,128]{3,2,1,0:T(8,128)}, f32[5,8,128]{2,1,0:T(8,128)S(1)}) custom-call(f32[2,5,5,16,16]{4,3,2,1,0:T(8,128)} %pad_maximum_fusion.2.sites_ref), custom_call_target="tpu_custom_call" | custom-call | tf_op jit(solution)/shard_map/mix_sites/pallas_call | solution.py:297
  123.9 5.2 %prep_lefts.1 = (bf16[2,5,96,768]{3,2,1,0:T(8,128)(2,1)}, f32[96,384]{1,0:T(8,128)}) custom-call(f32[4,96,384]{2,1,0:T(8,128)} %copy-done.1, f32[96,384]{1,0:T(8,128)} %collective-permute-done.9.beside_ref), custom_call_target="tpu_custom_call" | custom-call | tf_op jit(solution)/shard_map/prep_lefts/pallas_call | solution.py:338
  129.1 0.7 conditional.12
  129.1 0.7 copy.103
  129.7 1.3 collective-permute-start.10
  131.0 1.3 collective-permute-start.11
  132.4 1.6 slice_bitcast_fusion.2
  133.9 1.9 collective-permute-start.12
  135.9 5.7 %collective-permute-done.12 = f32[96,384]{1,0:T(8,128)} collective-permute-done((f32[96,384]{1,0:T(8,128)}, f32[96,384]{1,0:T(8,128)}, u32[]{:S(2)}, u32[]{:S(2)}) %collective-permute-start.12) | collective-permute-done | bytes 147488 | tf_op jit(solution)/shard_map/ppermute | solution.py:697
  141.6 0.7 conditional.13
  141.6 0.7 copy.107
  142.3 0.7 collective-permute-start.13
  143.0 1.3 collective-permute-start.14
  144.3 0.6 pad_add_fusion.place
  144.9 2.0 finish_terms.1
  146.9 87.0 %all-to-all-start.5 = ((f32[256,1,16]{2,1,0:T(1,128)}), f32[256,1,16]{2,1,0:T(1,128)S(1)}, u32[]{:S(2)}, u32[]{:S(2)}) async-start(f32[256,1,16]{2,1,0:T(1,128)} %bitcast.48), calls=%async_computation.5 | async-start | bytes 262144 | tf_op jit(solution)/shard_map/all_to_all | solution.py:753
  233.9 2.0 broadcast_select_fusion
  235.8 9.7 %all-to-all-done.5 = f32[256,1,16]{2,1,0:T(1,128)S(1)} async-done(((f32[256,1,16]{2,1,0:T(1,128)}), f32[256,1,16]{2,1,0:T(1,128)S(1)}, u32[]{:S(2)}, u32[]{:S(2)}) %all-to-all-start.5) | async-done | bytes 16416 | tf_op jit(solution)/shard_map/all_to_all | solution.py:753
  245.5 3.5 %all-to-all-start.4 = ((f32[4,96,384]{2,1,0:T(8,128)}), f32[4,96,384]{2,1,0:T(8,128)S(1)}, u32[]{:S(2)}, u32[]{:S(2)}) async-start(f32[4,96,384]{2,1,0:T(8,128)} %broadcast_select_fusion), calls=%async_computation.4 | async-start | bytes 1179648 | tf_op jit(solution)/shard_map/all_to_all | solution.py:743
  249.0 0.8 reduce_sum.9
  249.8 8.8 %all-to-all-done.4 = f32[4,96,384]{2,1,0:T(8,128)S(1)} async-done(((f32[4,96,384]{2,1,0:T(8,128)}), f32[4,96,384]{2,1,0:T(8,128)S(1)}, u32[]{:S(2)}, u32[]{:S(2)}) %all-to-all-start.4) | async-done | bytes 589856 | tf_op jit(solution)/shard_map/all_to_all | solution.py:743
  258.6 0.9 slice_bitcast_fusion
  (64 shorter events, 0.9 us)
Async XLA Ops:
  1.4 1.6 copy-start.2
  1.4 1.6 copy-start.3
  23.7 4.2 %copy-start = (f32[4,208,384]{2,1,0:T(8,128)}, f32[4,208,384]{2,1,0:T(8,128)S(1)}, u32[]{:S(2)}) copy-start(f32[4,208,384]{2,1,0:T(8,128)S(1)} %all_to_all.34.own_ref) | copy-start | bytes 3833860
  23.7 12.5 %copy-start.7 = (f32[2,96,384]{2,1,0:T(8,128)S(1)}, f32[2,96,384]{2,1,0:T(8,128)}, u32[]{:S(2)}) copy-start(f32[2,96,384]{2,1,0:T(8,128)} %param.30) | copy-start | bytes 884740
  23.7 12.5 %copy-start.8 = (f32[2,96,384]{2,1,0:T(8,128)S(1)}, f32[2,96,384]{2,1,0:T(8,128)}, u32[]{:S(2)}) copy-start(f32[2,96,384]{2,1,0:T(8,128)} %param.31) | copy-start | bytes 884740
  23.7 4.1 %collective-permute-start = (f32[4,208,384]{2,1,0:T(8,128)S(1)}, f32[4,208,384]{2,1,0:T(8,128)}, u32[]{:S(2)}, u32[]{:S(2)}) collective-permute-start(f32[4,208,384]{2,1,0:T(8,128)S(1)} %all_to_all.34.own_ref), channel_id=1, source_target_pairs={{0,8},{1,9},{2,10},{3,11},{4,12},{5,13},{6,14},{7,15},{16,24},{17,... | collective-permute-start | bytes 3833864 | tf_op jit(solution)/shard_map/ppermute | solution.py:631
  36.3 0.7 collective-permute-start.1
  37.0 1.5 copy-start.4
  37.0 1.5 copy-start.5
  37.0 4.3 %copy-start.10 = (s32[16]{0:T(128)S(1)}, s32[16]{0:T(128)}, u32[]{:S(2)}) copy-start(s32[16]{0:T(128)} %term_rows.1) | copy-start | bytes 196
  37.1 42.2 %copy-start.11 = (f32[4,96,384]{2,1,0:T(8,128)}, f32[4,96,384]{2,1,0:T(8,128)S(1)}, u32[]{:S(2)}) copy-start(f32[4,96,384]{2,1,0:T(8,128)S(1)} %get-tuple-element.307) | copy-start | bytes 1769476
  37.1 22.4 %collective-permute-start.3 = (f32[4,96,384]{2,1,0:T(8,128)S(1)}, f32[4,96,384]{2,1,0:T(8,128)S(1)}, u32[]{:S(2)}, u32[]{:S(2)}) collective-permute-start(f32[4,96,384]{2,1,0:T(8,128)S(1)} %get-tuple-element.307), channel_id=1, source_target_pairs={{8,0},{9,1},{10,2},{11,3},{12,4},{13,5},{14,6},{15,7},{24,16},{25,... | collective-permute-start | bytes 1769480 | tf_op jit(solution)/shard_map/ppermute | solution.py:594
  38.6 26.2 %collective-permute-start.6 = (f32[96,384]{1,0:T(8,128)S(1)}, f32[96,384]{1,0:T(8,128)S(1)}, u32[]{:S(2)}, u32[]{:S(2)}) collective-permute-start(f32[96,384]{1,0:T(8,128)S(1)} %select_bitcast_fusion.1), channel_id=1, source_target_pairs={{0,32},{64,96},{161,129},{225,193},{2,34},{66,98},{163,131},{227,1... | collective-permute-start | bytes 442376 | tf_op jit(solution)/shard_map/ppermute | solution.py:675
  59.4 5.0 %copy-start.9 = (s32[16]{0:T(128)S(1)}, s32[16]{0:T(128)}, u32[]{:S(2)}) copy-start(s32[16]{0:T(128)} %term_bonds.1) | copy-start | bytes 196
  60.3 15.0 %all-to-all-start.1 = ((f32[4,96,384]{2,1,0:T(8,128)}), f32[4,96,384]{2,1,0:T(8,128)}, u32[]{:S(2)}, u32[]{:S(2)}) async-start(f32[4,96,384]{2,1,0:T(8,128)} %broadcast_select_fusion.2), calls=%async_computation.1 | async-start | bytes 1179648 | tf_op jit(solution)/shard_map/all_to_all | solution.py:684
  66.7 12.5 %collective-permute-start.2 = (f32[96,384]{1,0:T(8,128)S(1)}, f32[96,384]{1,0:T(8,128)S(1)}, u32[]{:S(2)}, u32[]{:S(2)}) collective-permute-start(f32[96,384]{1,0:T(8,128)S(1)} %get-tuple-element.311), channel_id=1, source_target_pairs={{72,136},{168,104},{73,137},{169,105},{74,138},{170,106},{75,139},... | collective-permute-start | bytes 442376 | tf_op jit(solution)/shard_map/ppermute | solution.py:656
  75.3 8.6 %all-to-all-start.2 = ((f32[4,8,128]{2,1,0:T(8,128)}), f32[4,8,128]{2,1,0:T(8,128)S(1)}, u32[]{:S(2)}, u32[]{:S(2)}) async-start(f32[4,8,128]{2,1,0:T(8,128)} %reshape.66), calls=%async_computation.2 | async-start | bytes 32768 | tf_op jit(solution)/shard_map/all_to_all | solution.py:662
  79.3 9.0 %collective-permute-start.4 = (f32[96,384]{1,0:T(8,128)S(1)}, f32[96,384]{1,0:T(8,128)S(1)}, u32[]{:S(2)}, u32[]{:S(2)}) collective-permute-start(f32[96,384]{1,0:T(8,128)S(1)} %get-tuple-element.317), channel_id=1, source_target_pairs={{136,200},{104,40},{137,201},{105,41},{138,202},{106,42},{139,203}... | collective-permute-start | bytes 442376 | tf_op jit(solution)/shard_map/ppermute | solution.py:656
  83.9 5.8 %collective-permute-start.5 = (f32[8,128]{1,0:T(8,128)S(1)}, f32[8,128]{1,0:T(8,128)S(1)}, u32[]{:S(2)}, u32[]{:S(2)}) collective-permute-start(f32[8,128]{1,0:T(8,128)S(1)} %slice_bitcast_fusion.4), channel_id=1, source_target_pairs={{2,0},{4,2},{6,4},{3,1},{5,3},{7,5},{10,8},{12,10},{14,12},{11,9},... | collective-permute-start | bytes 12296 | tf_op jit(solution)/shard_map/ppermute | solution.py:663
  86.9 12.5 %collective-permute-start.8 = (f32[4,96,384]{2,1,0:T(8,128)}, f32[4,96,384]{2,1,0:T(8,128)S(1)}, u32[]{:S(2)}, u32[]{:S(2)}) collective-permute-start(f32[4,96,384]{2,1,0:T(8,128)} %all-to-all-done.1), channel_id=1, source_target_pairs={{0,32},{64,96},{160,128},{224,192},{1,33},{65,97},{161,129},{225,1... | collective-permute-start | bytes 1769480 | tf_op jit(solution)/shard_map/ppermute | solution.py:686
  88.3 11.1 %collective-permute-start.7 = (f32[4,96,384]{2,1,0:T(8,128)}, f32[4,96,384]{2,1,0:T(8,128)S(1)}, u32[]{:S(2)}, u32[]{:S(2)}) collective-permute-start(f32[4,96,384]{2,1,0:T(8,128)} %get-tuple-element.318), channel_id=1, source_target_pairs={{8,0},{9,1},{10,2},{11,3},{12,4},{13,5},{14,6},{15,7},{24,16},{25,... | collective-permute-start | bytes 1769480 | tf_op jit(solution)/shard_map/ppermute | solution.py:594
  99.4 5.2 %copy-start.1 = (f32[4,96,384]{2,1,0:T(8,128)}, f32[4,96,384]{2,1,0:T(8,128)S(1)}, u32[]{:S(2)}) copy-start(f32[4,96,384]{2,1,0:T(8,128)S(1)} %collective-permute-done.8.cols_ref) | copy-start | bytes 1769476
  100.4 28.7 %all-to-all-start.3 = ((f32[4,96,384]{2,1,0:T(8,128)}), f32[4,96,384]{2,1,0:T(8,128)}, u32[]{:S(2)}, u32[]{:S(2)}) async-start(f32[4,96,384]{2,1,0:T(8,128)} %broadcast_select_fusion.1), calls=%async_computation.3 | async-start | bytes 1179648 | tf_op jit(solution)/shard_map/all_to_all | solution.py:693
  105.2 18.6 %collective-permute-start.9 = (f32[96,384]{1,0:T(8,128)}, f32[96,384]{1,0:T(8,128)}, u32[]{:S(2)}, u32[]{:S(2)}) collective-permute-start(f32[96,384]{1,0:T(8,128)} %slice_bitcast_fusion.3), channel_id=1, source_target_pairs={{2,0},{4,2},{6,4},{3,1},{5,3},{7,5},{10,8},{12,10},{14,12},{11,9},... | collective-permute-start | bytes 442376 | tf_op jit(solution)/shard_map/ppermute | solution.py:695
  129.7 104.1 %collective-permute-start.10 = (f32[4,96,384]{2,1,0:T(8,128)}, f32[4,96,384]{2,1,0:T(8,128)}, u32[]{:S(2)}, u32[]{:S(2)}) collective-permute-start(f32[4,96,384]{2,1,0:T(8,128)} %get-tuple-element.329), channel_id=1, source_target_pairs={{8,0},{9,1},{10,2},{11,3},{12,4},{13,5},{14,6},{15,7},{24,16},{25,... | collective-permute-start | bytes 1769480 | tf_op jit(solution)/shard_map/ppermute | solution.py:594
  131.0 4.8 %collective-permute-start.11 = (f32[96,384]{1,0:T(8,128)}, f32[96,384]{1,0:T(8,128)}, u32[]{:S(2)}, u32[]{:S(2)}) collective-permute-start(f32[96,384]{1,0:T(8,128)} %get-tuple-element.332), channel_id=1, source_target_pairs={{32,34},{38,36},{96,98},{102,100},{128,130},{134,132},{192,194},{1... | collective-permute-start | bytes 442376 | tf_op jit(solution)/shard_map/ppermute | solution.py:735
  133.9 7.7 %collective-permute-start.12 = (f32[96,384]{1,0:T(8,128)}, f32[96,384]{1,0:T(8,128)}, u32[]{:S(2)}, u32[]{:S(2)}) collective-permute-start(f32[96,384]{1,0:T(8,128)} %slice_bitcast_fusion.2), channel_id=1, source_target_pairs={{2,0},{4,2},{6,4},{3,1},{5,3},{7,5},{10,8},{12,10},{14,12},{11,9},... | collective-permute-start | bytes 442376 | tf_op jit(solution)/shard_map/ppermute | solution.py:697
  142.3 0.7 collective-permute-start.13
  143.0 1.9 collective-permute-start.14
  146.9 98.6 %all-to-all-start.5 = ((f32[256,1,16]{2,1,0:T(1,128)}), f32[256,1,16]{2,1,0:T(1,128)S(1)}, u32[]{:S(2)}, u32[]{:S(2)}) async-start(f32[256,1,16]{2,1,0:T(1,128)} %bitcast.48), calls=%async_computation.5 | async-start | bytes 262144 | tf_op jit(solution)/shard_map/all_to_all | solution.py:753
  245.5 13.1 %all-to-all-start.4 = ((f32[4,96,384]{2,1,0:T(8,128)}), f32[4,96,384]{2,1,0:T(8,128)S(1)}, u32[]{:S(2)}, u32[]{:S(2)}) async-start(f32[4,96,384]{2,1,0:T(8,128)} %broadcast_select_fusion), calls=%async_computation.4 | async-start | bytes 1179648 | tf_op jit(solution)/shard_map/all_to_all | solution.py:743
where the time goes:
time: 262 us; the launch traced here: 259 us
  starting transfers between devices  124 us (47%)
  waiting for transfers between devices  64.9 us (25%)
  Pallas kernels  24.5 us (9%)
  blocking collectives  20.6 us (8%)
  local copies, waits for them, and re-layouts  15.6 us (6%)
  other arithmetic  8.31 us (3%)
    all_to_all x1, starting transfers between devices, shards(): energies = jnp.sum(lax.all_to_all(shares, BLOCK, 0, 0), axis=0)  87 us
    all_to_all x1, blocking collectives, shards(): lax.all_to_all(payload.reshape(4, 2 * CHI + 16, 4 * CHI), ('zz', 'xl'), 0...  20.6 us
    ppermute x3, waiting for transfers between devices, core_shared(): return jnp.where(core == 1, odd, lax.ppermute(even, 'co', [(1, 0)]))  18.1 us
    all_to_all x1, waiting for transfers between devices, shards(): energies = jnp.sum(lax.all_to_all(shares, BLOCK, 0, 0), axis=0)  9.68 us
    ppermute x1, waiting for transfers between devices, shards(): early = lax.ppermute(early, ('b', 'zz'), [(0, 1), (2, 3), (5, 4), (7, 6)])  9.16 us
    pallas_call x1, Pallas kernels, mix_sites(): pl.pallas_call(mix_sites_body, grid=(5,), in_specs=[pl.BlockSpec((2, 1, 5...  8.89 us
    all_to_all x1, waiting for transfers between devices, shards(): lax.all_to_all(core_shared(rows[2], rows[3], core), ('zz', 'xl'), 0, 0)  8.81 us
    pallas_call x1, Pallas kernels, prep_maps(): pl.pallas_call(prep_body, grid=(4,), in_specs=[block, block], out_specs=[...  8.38 us
  transfers between devices with their start and end apart: 20, of which 8 were waited for; matrix products, arithmetic and copies ran while one was open for 7% of the time, Pallas kernels for 6%

commit v1 on v0

--- a/solution.py
+++ b/solution.py
@@ -117,9 +117,7 @@
 PACKED = MIXER_ROW + LANES
 
 
-def prep_body(own_ref, other_ref, maps_ref, *rest):
-    deal_ref, dense_ref = rest[-2:]
-
+def prep_body(rows_ref, maps_ref, deal_ref, dense_ref):
     @pl.when(pl.program_id(0) == 0)
     def _():
         deal_ref[...] = one_hot(
@@ -129,39 +127,46 @@
             4 * CHI, 4 * CHI, lambda r, c: (r & 3 == (c >> 3) & 3) & (r >> 2 == (c >> 5) * 8 + (c & 7))
         )
 
-    deal = deal_ref[...]
-    dense = dense_ref[...]
     blank = jnp.zeros((LANES - CHI, 3 * LANES), BF16)
-    refs = (other_ref, own_ref)
-    parts = [part for ref in refs for part in split_three(ref[0, 0:CHI, :])]
-    lefts = dot(jnp.concatenate(parts, axis=0), dense).astype(BF16)
-    parts = [part for ref in refs for part in split_three(ref[0, CHI : 2 * CHI, :])]
-    rights = dot(jnp.concatenate(parts, axis=0), deal).astype(BF16)
-    for parity, ref in enumerate(refs):
-        maps_ref[parity, LEFT_ROW:MIXER_ROW, :] = lefts[parity * 3 * CHI : (parity + 1) * 3 * CHI]
+    parts = [part for spot in range(2) for part in split_three(rows_ref[spot, 0:CHI, :])]
+    lefts = dot(jnp.concatenate(parts, axis=0), dense_ref[...]).astype(BF16)
+    parts = [part for spot in range(2) for part in split_three(rows_ref[spot, CHI : 2 * CHI, :])]
+    rights = dot(jnp.concatenate(parts, axis=0), deal_ref[...]).astype(BF16)
+    for spot in range(2):
+        maps_ref[spot, LEFT_ROW:MIXER_ROW, :] = lefts[spot * 3 * CHI : (spot + 1) * 3 * CHI]
         for j in range(D2):
-            starts = [(parity * 3 + part) * CHI for part in range(3)]
-            maps_ref[parity, j * LANES : j * LANES + CHI, :] = jnp.concatenate(
+            starts = [(spot * 3 + part) * CHI for part in range(3)]
+            maps_ref[spot, j * LANES : j * LANES + CHI, :] = jnp.concatenate(
                 [rights[start : start + CHI, j * LANES : (j + 1) * LANES] for start in starts], axis=1
             )
-            maps_ref[parity, j * LANES + CHI : (j + 1) * LANES, :] = blank
-        maps_ref[parity, MIXER_ROW:PACKED, :] = expand_mixer(ref[0, 2 * CHI :, 0:16])
-
-
-def prep_maps(own, other):
-    block = pl.BlockSpec((1, 2 * CHI + 16, 4 * CHI), lambda t: (t, 0, 0))
-    unwritten = jax.ShapeDtypeStruct((4, CHI, 4 * CHI), F32)
+            maps_ref[spot, j * LANES + CHI : (j + 1) * LANES, :] = blank
+        maps_ref[spot, MIXER_ROW:PACKED, :] = expand_mixer(rows_ref[spot, 2 * CHI :, 0:16])
+
+
+def prep_maps(rows):
     return pl.pallas_call(
         prep_body,
-        grid=(4,),
-        in_specs=[block, block],
-        out_specs=[pl.BlockSpec((2, PACKED, 4 * CHI), lambda t: (t, 0, 0))] + [pl.BlockSpec(memory_space=pl.ANY)] * 5,
-        out_shape=[jax.ShapeDtypeStruct((8, PACKED, 4 * CHI), BF16)]
-        + [unwritten] * 4
-        + [jax.ShapeDtypeStruct((CHI, 4 * CHI), F32)],
+        grid=(2,),
+        in_specs=[pl.BlockSpec((2, 2 * CHI + 16, 4 * CHI), lambda t: (t, 0, 0))],
+        out_specs=pl.BlockSpec((2, PACKED, 4 * CHI), lambda t: (t, 0, 0)),
+        out_shape=jax.ShapeDtypeStruct((4, PACKED, 4 * CHI), BF16),
         scratch_shapes=[pltpu.VMEM((4 * CHI, D2 * LANES), BF16), pltpu.VMEM((4 * CHI, 4 * CHI), BF16)],
         name="prep_maps",
-    )(own, other)
+    )(rows)
+
+
+def blank_body(*blanks):
+    pass
+
+
+def blank_rows():
+    rows = jax.ShapeDtypeStruct((4, CHI, 4 * CHI), F32)
+    return pl.pallas_call(
+        blank_body,
+        out_specs=[pl.BlockSpec(memory_space=pl.ANY)] * 5,
+        out_shape=[rows] * 4 + [jax.ShapeDtypeStruct((CHI, 4 * CHI), F32)],
+        name="blank_rows",
+    )()
 
 
 def load_state(state_ref, flat):
@@ -185,7 +190,8 @@
 def chain_body(
     upward,
     start_ref,
-    maps_ref,
+    even_maps,
+    odd_maps,
     fed_even,
     fed_odd,
     made_even,
@@ -201,13 +207,22 @@
     def row_of(step):
         return jnp.where(upward[0] == 1, 7 - step, step)
 
-    def fetch(step, slot):
-        return pltpu.make_async_copy(maps_ref.at[row_of(step)], slots_ref.at[slot], slot_sems.at[slot])
+    def fetch(source, step, slot):
+        return pltpu.make_async_copy(source.at[row_of(step) >> 1], slots_ref.at[slot], slot_sems.at[slot])
+
+    def start_fetch(step, slot):
+        @pl.when(row_of(step) & 1 == 0)
+        def _():
+            fetch(even_maps, step, slot).start()
+
+        @pl.when(row_of(step) & 1 == 1)
+        def _():
+            fetch(odd_maps, step, slot).start()
 
     def send(target, step, row, sems):
         return pltpu.make_async_copy(flats_ref.at[step], target.at[row >> 1], sems.at[row])
 
-    fetch(0, 0).start()
+    start_fetch(0, 0)
     state_ref[...] = jnp.zeros_like(state_ref)
     load_state(state_ref, start_ref[...])
 
@@ -235,9 +250,9 @@
 
         @pl.when(step < 7)
         def _():
-            fetch(step + 1, 1 - slot).start()
-
-        fetch(step, slot).wait()
+            start_fetch(step + 1, 1 - slot)
+
+        fetch(even_maps, step, slot).wait()
         state, scale = scaled_state(step)
         maps = slots_ref.at[slot]
         rights = [maps[0:LEFT_ROW, part * LANES : (part + 1) * LANES] for part in range(3)]
@@ -261,13 +276,13 @@
         send(made_odd if row & 1 else made_even, 0, row, made_sems).wait()
 
 
-def run_chain(upward, start, maps):
+def run_chain(upward, start, even_maps, odd_maps):
     flat_spec = pl.BlockSpec((CHI, 4 * CHI), lambda step, up: (0, 0))
     anywhere = pl.BlockSpec(memory_space=pl.ANY)
     grid_spec = pltpu.PrefetchScalarGridSpec(
         num_scalar_prefetch=1,
         grid=(1,),
-        in_specs=[flat_spec, anywhere],
+        in_specs=[flat_spec, anywhere, anywhere],
         out_specs=[anywhere, anywhere, anywhere, anywhere, flat_spec],
         scratch_shapes=[
             pltpu.VMEM((4 * CHI, LANES), F32),
@@ -284,7 +299,7 @@
         grid_spec=grid_spec,
         out_shape=[rows, rows, rows, rows, jax.ShapeDtypeStruct((CHI, 4 * CHI), F32)],
         name="run_chain",
-    )(upward, start, maps)
+    )(upward, start, even_maps, odd_maps)
 
 
 def mix_sites_body(sites_ref, mixers_ref, opens_ref, rho_ref):
@@ -629,7 +644,9 @@
     payload = jnp.concatenate([left_maps[:, 0], right_maps[:, 0], extra], axis=2)
     own = lax.all_to_all(payload.reshape(4, 2 * CHI + 16, 4 * CHI), ("zz", "xl"), 0, 0)
     other = lax.ppermute(own, "co", [(0, 1)])
-    maps, *rows, unused = prep_maps(own, other)
+    odd_maps = prep_maps(own)
+    even_maps = prep_maps(other)
+    *rows, unused = blank_rows()
 
     start = jnp.where(
         upward == 0,
@@ -643,7 +660,7 @@
     def run_stage(k, source, rows):
         *rows, last = lax.cond(
             (stage == k) & (core == 1),
-            lambda source, unused, *rows: tuple(run_chain(direction, source, maps)),
+            lambda source, unused, *rows: tuple(run_chain(direction, source, even_maps, odd_maps)),
             lambda source, unused, *rows: rows + (unused,),
             source,
             unused,

time: 262 us -> 264 us (level)
  waiting for transfers between devices: 64.9 us -> 60.2 us
    pallas_call x1 -> x3, Pallas kernels: 8.38 us -> 9.57 us  [the longest x2 9.57 us: prep_maps(): pl.pallas_call(prep_body, grid=(2,), in_specs=[pl.BlockSpec((2, 2 * CHI +...]
  transfers between devices with their start and end apart: 20 -> 20, of which waited for: 8 -> 7; matrix products, arithmetic and copies ran while one was open for 7% -> 8% of each run, Pallas kernels for 6% -> 8%
where the time goes in v1:
time: 264 us; the launch traced here: 261 us
  starting transfers between devices  126 us (48%)
  waiting for transfers between devices  60.2 us (23%)
  Pallas kernels  25.7 us (10%)
  blocking collectives  20.7 us (8%)
  local copies, waits for them, and re-layouts  17.7 us (7%)
  other arithmetic  9.32 us (4%)
    all_to_all x1, starting transfers between devices, shards(): energies = jnp.sum(lax.all_to_all(shares, BLOCK, 0, 0), axis=0)  87.6 us
    all_to_all x1, blocking collectives, shards(): lax.all_to_all(payload.reshape(4, 2 * CHI + 16, 4 * CHI), ('zz', 'xl'), 0...  20.7 us
    ppermute x3, waiting for transfers between devices, core_shared(): return jnp.where(core == 1, odd, lax.ppermute(even, 'co', [(1, 0)]))  16.3 us
    all_to_all x1, waiting for transfers between devices, shards(): energies = jnp.sum(lax.all_to_all(shares, BLOCK, 0, 0), axis=0)  9.67 us
    pallas_call x2, Pallas kernels, prep_maps(): pl.pallas_call(prep_body, grid=(2,), in_specs=[pl.BlockSpec((2, 2 * CHI +...  9.57 us
    pallas_call x1, Pallas kernels, mix_sites(): pl.pallas_call(mix_sites_body, grid=(5,), in_specs=[pl.BlockSpec((2, 1, 5...  8.89 us
    all_to_all x1, waiting for transfers between devices, shards(): lax.all_to_all(core_shared(rows[2], rows[3], core), ('zz', 'xl'), 0, 0)  8.81 us
    ppermute x1, waiting for transfers between devices, shards(): early = lax.ppermute(early, ('b', 'zz'), [(0, 1), (2, 3), (5, 4), (7, 6)])  8.69 us
  transfers between devices with their start and end apart: 20, of which 7 were waited for; matrix products, arithmetic and copies ran while one was open for 8% of the time, Pallas kernels for 8%

profile of v1, /device:TPU:8, one launch (start us, length us, event | category | flops | bytes accessed | tf_op | source)
XLA Modules:
  0.0 261.0 jit_solution(2090829928898182779)
XLA Ops:
  0.6 0.8 mul.35
  1.4 0.2 broadcast_multiply_fusion
  1.6 0.7 mul.40
  2.3 0.4 reshape.70
  3.1 20.7 %all_to_all.34.rows_ref = f32[4,208,384]{2,1,0:T(8,128)} all-to-all(f32[4,208,384]{2,1,0:T(8,128)S(1)} %pad_maximum_fusion), channel_id=1, replica_groups=mesh['b'=4,'zz'=2,'xl'=2,'co'=2,'y'=4,'xh'=2] {'zz','xl'}, dimensions={0} | all-to-all | bytes 2555904 | tf_op jit(solution)/shard_map/all_to_all | solution.py:645
  23.8 2.4 collective-permute-start
  26.2 4.2 %prep_maps.3 = bf16[4,928,384]{2,1,0:T(8,128)(2,1)S(1)} custom-call(f32[4,208,384]{2,1,0:T(8,128)} %all_to_all.34.rows_ref), custom_call_target="tpu_custom_call" | custom-call | tf_op jit(solution)/shard_map/prep_maps/pallas_call | solution.py:147
  30.4 5.3 %prep_maps.2 = bf16[4,928,384]{2,1,0:T(8,128)(2,1)} custom-call(f32[4,208,384]{2,1,0:T(8,128)} %collective-permute-done.rows_ref), custom_call_target="tpu_custom_call" | custom-call | tf_op jit(solution)/shard_map/prep_maps/pallas_call | solution.py:147
  35.8 0.7 collective-permute-start.1
  36.5 0.7 conditional.9
  36.6 0.7 copy.77
  37.2 1.3 collective-permute-start.3
  38.6 2.7 %collective-permute-start.6 = (f32[96,384]{1,0:T(8,128)S(1)}, f32[96,384]{1,0:T(8,128)S(1)}, u32[]{:S(2)}, u32[]{:S(2)}) collective-permute-start(f32[96,384]{1,0:T(8,128)S(1)} %select_bitcast_fusion.1), channel_id=1, source_target_pairs={{0,32},{64,96},{161,129},{225,193},{2,34},{66,98},{163,131},{227,1... | collective-permute-start | bytes 442376 | tf_op jit(solution)/shard_map/ppermute | solution.py:692
  41.4 16.2 %collective-permute-done.3 = f32[4,96,384]{2,1,0:T(8,128)} collective-permute-done((f32[4,96,384]{2,1,0:T(8,128)}, f32[4,96,384]{2,1,0:T(8,128)}, u32[]{:S(2)}, u32[]{:S(2)}) %collective-permute-start.3) | collective-permute-done | bytes 589856 | tf_op jit(solution)/shard_map/ppermute | solution.py:609
  57.6 2.0 broadcast_select_fusion.2
  59.6 4.2 %all-to-all-start.1 = ((f32[4,96,384]{2,1,0:T(8,128)}), f32[4,96,384]{2,1,0:T(8,128)}, u32[]{:S(2)}, u32[]{:S(2)}) async-start(f32[4,96,384]{2,1,0:T(8,128)} %broadcast_select_fusion.2), calls=%async_computation.1 | async-start | bytes 1179648 | tf_op jit(solution)/shard_map/all_to_all | solution.py:701
  64.6 0.8 slice.50
  65.3 0.7 reshape.66
  66.0 0.7 collective-permute-start.2
  66.7 8.2 %all-to-all-done.1 = f32[4,96,384]{2,1,0:T(8,128)} async-done(((f32[4,96,384]{2,1,0:T(8,128)}), f32[4,96,384]{2,1,0:T(8,128)}, u32[]{:S(2)}, u32[]{:S(2)}) %all-to-all-start.1) | async-done | bytes 589856 | tf_op jit(solution)/shard_map/all_to_all | solution.py:701
  74.9 3.2 %all-to-all-start.2 = ((f32[4,8,128]{2,1,0:T(8,128)}), f32[4,8,128]{2,1,0:T(8,128)S(1)}, u32[]{:S(2)}, u32[]{:S(2)}) async-start(f32[4,8,128]{2,1,0:T(8,128)} %reshape.66), calls=%async_computation.2 | async-start | bytes 32768 | tf_op jit(solution)/shard_map/all_to_all | solution.py:679
  78.1 0.7 broadcast_select_fusion.4
  78.8 0.7 conditional.10
  78.8 0.7 copy.87
  79.5 1.3 collective-permute-start.4
  80.8 2.7 %all-to-all-done.2 = f32[4,8,128]{2,1,0:T(8,128)S(1)} async-done(((f32[4,8,128]{2,1,0:T(8,128)}), f32[4,8,128]{2,1,0:T(8,128)S(1)}, u32[]{:S(2)}, u32[]{:S(2)}) %all-to-all-start.2) | async-done | bytes 16416 | tf_op jit(solution)/shard_map/all_to_all | solution.py:679
  83.5 2.3 collective-permute-start.5
  85.8 0.7 concatenate.35
  86.5 2.1 collective-permute-start.8
  88.6 1.3 collective-permute-start.7
  90.2 0.3 pad_maximum_fusion.1
  90.6 8.7 %collective-permute-done.8.cols_ref = f32[4,96,384]{2,1,0:T(8,128)} collective-permute-done((f32[4,96,384]{2,1,0:T(8,128)}, f32[4,96,384]{2,1,0:T(8,128)}, u32[]{:S(2)}, u32[]{:S(2)}) %collective-permute-start.8) | collective-permute-done | bytes 589856 | tf_op jit(solution)/shard_map/ppermute | solution.py:703
  99.3 0.9 broadcast_select_fusion.1
  100.2 4.3 %all-to-all-start.3 = ((f32[4,96,384]{2,1,0:T(8,128)}), f32[4,96,384]{2,1,0:T(8,128)}, u32[]{:S(2)}, u32[]{:S(2)}) async-start(f32[4,96,384]{2,1,0:T(8,128)} %broadcast_select_fusion.1), calls=%async_computation.3 | async-start | bytes 1179648 | tf_op jit(solution)/shard_map/all_to_all | solution.py:710
  104.5 1.6 slice_bitcast_fusion.3
  106.1 1.9 collective-permute-start.9
  108.0 0.6 fusion.1
  108.7 2.7 %copy.40 = f32[5,5,4,4,4,4]{5,4,3,2,1,0:T(4,128)S(1)} copy(f32[5,5,4,4,4,4]{4,5,3,2,1,0:T(4,128)S(1)} %get-tuple-element.346) | data formatting | bytes 51200 | tf_op jit(solution)/shard_map/transpose | solution.py:687
  111.4 0.4 stack_reshape.15
  111.8 2.7 %copy.39 = f32[5,5,4,4,4,4]{5,4,3,2,1,0:T(4,128)S(1)} copy(f32[5,5,4,4,4,4]{3,5,4,2,1,0:T(4,128)S(1)} %get-tuple-element.345) | data formatting | bytes 51200 | tf_op jit(solution)/shard_map/transpose | solution.py:686
  114.5 0.4 stack_reshape.14
  114.9 0.8 pad_maximum_fusion.2.sites_ref
  115.6 8.9 %mix_sites.1 = (bf16[2,5,5,128,256]{4,3,2,1,0:T(8,128)(2,1)S(1)}, f32[4,4,384,128]{3,2,1,0:T(8,128)}, f32[5,8,128]{2,1,0:T(8,128)S(1)}) custom-call(f32[2,5,5,16,16]{4,3,2,1,0:T(8,128)} %pad_maximum_fusion.2.sites_ref), custom_call_target="tpu_custom_call" | custom-call | tf_op jit(solution)/shard_map/mix_sites/pallas_call | solution.py:312
  124.6 5.2 %prep_lefts.1 = (bf16[2,5,96,768]{3,2,1,0:T(8,128)(2,1)}, f32[96,384]{1,0:T(8,128)}) custom-call(f32[4,96,384]{2,1,0:T(8,128)} %collective-permute-done.8.cols_ref, f32[96,384]{1,0:T(8,128)} %collective-permute-done.9.beside_ref), custom_call_target="tpu_custom_call" | custom-call | tf_op jit(solution)/shard_map/prep_lefts/pallas_call | solution.py:353
  129.7 0.7 conditional.12
  129.7 0.7 copy.103
  130.4 1.3 collective-permute-start.10
  131.7 1.3 collective-permute-start.11
  133.0 1.6 slice_bitcast_fusion.2
  134.6 1.9 collective-permute-start.12
  136.5 5.9 %collective-permute-done.12 = f32[96,384]{1,0:T(8,128)} collective-permute-done((f32[96,384]{1,0:T(8,128)}, f32[96,384]{1,0:T(8,128)}, u32[]{:S(2)}, u32[]{:S(2)}) %collective-permute-start.12) | collective-permute-done | bytes 147488 | tf_op jit(solution)/shard_map/ppermute | solution.py:714
  142.5 0.7 conditional.13
  142.5 0.7 copy.107
  143.1 0.7 collective-permute-start.13
  143.8 1.3 collective-permute-start.14
  145.1 0.6 pad_add_fusion.place
  145.7 2.0 finish_terms.1
  147.8 87.6 %all-to-all-start.5 = ((f32[256,1,16]{2,1,0:T(1,128)}), f32[256,1,16]{2,1,0:T(1,128)S(1)}, u32[]{:S(2)}, u32[]{:S(2)}) async-start(f32[256,1,16]{2,1,0:T(1,128)} %bitcast.48), calls=%async_computation.5 | async-start | bytes 262144 | tf_op jit(solution)/shard_map/all_to_all | solution.py:770
  235.4 2.0 broadcast_select_fusion
  237.4 9.7 %all-to-all-done.5 = f32[256,1,16]{2,1,0:T(1,128)S(1)} async-done(((f32[256,1,16]{2,1,0:T(1,128)}), f32[256,1,16]{2,1,0:T(1,128)S(1)}, u32[]{:S(2)}, u32[]{:S(2)}) %all-to-all-start.5) | async-done | bytes 16416 | tf_op jit(solution)/shard_map/all_to_all | solution.py:770
  247.0 3.5 %all-to-all-start.4 = ((f32[4,96,384]{2,1,0:T(8,128)}), f32[4,96,384]{2,1,0:T(8,128)S(1)}, u32[]{:S(2)}, u32[]{:S(2)}) async-start(f32[4,96,384]{2,1,0:T(8,128)} %broadcast_select_fusion), calls=%async_computation.4 | async-start | bytes 1179648 | tf_op jit(solution)/shard_map/all_to_all | solution.py:760
  250.5 0.8 reduce_sum.9
  251.3 8.8 %all-to-all-done.4 = f32[4,96,384]{2,1,0:T(8,128)S(1)} async-done(((f32[4,96,384]{2,1,0:T(8,128)}), f32[4,96,384]{2,1,0:T(8,128)S(1)}, u32[]{:S(2)}, u32[]{:S(2)}) %all-to-all-start.4) | async-done | bytes 589856 | tf_op jit(solution)/shard_map/all_to_all | solution.py:760
  260.1 0.9 slice_bitcast_fusion
  (56 shorter events, 1.5 us)
Async XLA Ops:
  1.4 1.6 copy-start.1
  1.4 1.6 copy-start.2
  23.8 6.6 %collective-permute-start = (f32[4,208,384]{2,1,0:T(8,128)}, f32[4,208,384]{2,1,0:T(8,128)}, u32[]{:S(2)}, u32[]{:S(2)}) collective-permute-start(f32[4,208,384]{2,1,0:T(8,128)} %all_to_all.34.rows_ref), channel_id=1, source_target_pairs={{0,8},{1,9},{2,10},{3,11},{4,12},{5,13},{6,14},{7,15},{16,24},{17,... | collective-permute-start | bytes 3833864 | tf_op jit(solution)/shard_map/ppermute | solution.py:646
  35.8 0.7 collective-permute-start.1
  36.5 2.0 copy-start.3
  36.5 4.8 %copy-start.6 = (s32[16]{0:T(128)S(1)}, s32[16]{0:T(128)}, u32[]{:S(2)}) copy-start(s32[16]{0:T(128)} %term_rows.1) | copy-start | bytes 196
  37.2 20.4 %collective-permute-start.3 = (f32[4,96,384]{2,1,0:T(8,128)}, f32[4,96,384]{2,1,0:T(8,128)}, u32[]{:S(2)}, u32[]{:S(2)}) collective-permute-start(f32[4,96,384]{2,1,0:T(8,128)} %get-tuple-element.311), channel_id=1, source_target_pairs={{8,0},{9,1},{10,2},{11,3},{12,4},{13,5},{14,6},{15,7},{24,16},{25,... | collective-permute-start | bytes 1769480 | tf_op jit(solution)/shard_map/ppermute | solution.py:609
  38.6 25.5 %collective-permute-start.6 = (f32[96,384]{1,0:T(8,128)S(1)}, f32[96,384]{1,0:T(8,128)S(1)}, u32[]{:S(2)}, u32[]{:S(2)}) collective-permute-start(f32[96,384]{1,0:T(8,128)S(1)} %select_bitcast_fusion.1), channel_id=1, source_target_pairs={{0,32},{64,96},{161,129},{225,193},{2,34},{66,98},{163,131},{227,1... | collective-permute-start | bytes 442376 | tf_op jit(solution)/shard_map/ppermute | solution.py:692
  57.6 6.1 %copy-start.5 = (s32[16]{0:T(128)S(1)}, s32[16]{0:T(128)}, u32[]{:S(2)}) copy-start(s32[16]{0:T(128)} %term_bonds.1) | copy-start | bytes 196
  59.6 15.3 %all-to-all-start.1 = ((f32[4,96,384]{2,1,0:T(8,128)}), f32[4,96,384]{2,1,0:T(8,128)}, u32[]{:S(2)}, u32[]{:S(2)}) async-start(f32[4,96,384]{2,1,0:T(8,128)} %broadcast_select_fusion.2), calls=%async_computation.1 | async-start | bytes 1179648 | tf_op jit(solution)/shard_map/all_to_all | solution.py:701
  66.0 12.8 %collective-permute-start.2 = (f32[96,384]{1,0:T(8,128)}, f32[96,384]{1,0:T(8,128)S(1)}, u32[]{:S(2)}, u32[]{:S(2)}) collective-permute-start(f32[96,384]{1,0:T(8,128)} %get-tuple-element.315), channel_id=1, source_target_pairs={{72,136},{168,104},{73,137},{169,105},{74,138},{170,106},{75,139},... | collective-permute-start | bytes 442376 | tf_op jit(solution)/shard_map/ppermute | solution.py:673
  74.9 8.6 %all-to-all-start.2 = ((f32[4,8,128]{2,1,0:T(8,128)}), f32[4,8,128]{2,1,0:T(8,128)S(1)}, u32[]{:S(2)}, u32[]{:S(2)}) async-start(f32[4,8,128]{2,1,0:T(8,128)} %reshape.66), calls=%async_computation.2 | async-start | bytes 32768 | tf_op jit(solution)/shard_map/all_to_all | solution.py:679
  79.5 9.1 %collective-permute-start.4 = (f32[96,384]{1,0:T(8,128)}, f32[96,384]{1,0:T(8,128)}, u32[]{:S(2)}, u32[]{:S(2)}) collective-permute-start(f32[96,384]{1,0:T(8,128)} %get-tuple-element.321), channel_id=1, source_target_pairs={{136,200},{104,40},{137,201},{105,41},{138,202},{106,42},{139,203}... | collective-permute-start | bytes 442376 | tf_op jit(solution)/shard_map/ppermute | solution.py:673
  83.5 6.5 %collective-permute-start.5 = (f32[8,128]{1,0:T(8,128)S(1)}, f32[8,128]{1,0:T(8,128)S(1)}, u32[]{:S(2)}, u32[]{:S(2)}) collective-permute-start(f32[8,128]{1,0:T(8,128)S(1)} %slice_bitcast_fusion.4), channel_id=1, source_target_pairs={{2,0},{4,2},{6,4},{3,1},{5,3},{7,5},{10,8},{12,10},{14,12},{11,9},... | collective-permute-start | bytes 12296 | tf_op jit(solution)/shard_map/ppermute | solution.py:680
  86.5 12.8 %collective-permute-start.8 = (f32[4,96,384]{2,1,0:T(8,128)}, f32[4,96,384]{2,1,0:T(8,128)}, u32[]{:S(2)}, u32[]{:S(2)}) collective-permute-start(f32[4,96,384]{2,1,0:T(8,128)} %all-to-all-done.1), channel_id=1, source_target_pairs={{0,32},{64,96},{160,128},{224,192},{1,33},{65,97},{161,129},{225,1... | collective-permute-start | bytes 1769480 | tf_op jit(solution)/shard_map/ppermute | solution.py:703
  88.6 10.6 %collective-permute-start.7 = (f32[4,96,384]{2,1,0:T(8,128)}, f32[4,96,384]{2,1,0:T(8,128)S(1)}, u32[]{:S(2)}, u32[]{:S(2)}) collective-permute-start(f32[4,96,384]{2,1,0:T(8,128)} %get-tuple-element.322), channel_id=1, source_target_pairs={{8,0},{9,1},{10,2},{11,3},{12,4},{13,5},{14,6},{15,7},{24,16},{25,... | collective-permute-start | bytes 1769480 | tf_op jit(solution)/shard_map/ppermute | solution.py:609
  90.0 9.3 %copy-start = (f32[4,96,384]{2,1,0:T(8,128)S(1)}, f32[4,96,384]{2,1,0:T(8,128)}, u32[]{:S(2)}) copy-start(f32[4,96,384]{2,1,0:T(8,128)} %get-tuple-element.323) | copy-start | bytes 1769476
  100.2 29.6 %all-to-all-start.3 = ((f32[4,96,384]{2,1,0:T(8,128)}), f32[4,96,384]{2,1,0:T(8,128)}, u32[]{:S(2)}, u32[]{:S(2)}) async-start(f32[4,96,384]{2,1,0:T(8,128)} %broadcast_select_fusion.1), calls=%async_computation.3 | async-start | bytes 1179648 | tf_op jit(solution)/shard_map/all_to_all | solution.py:710
  106.1 18.5 %collective-permute-start.9 = (f32[96,384]{1,0:T(8,128)}, f32[96,384]{1,0:T(8,128)}, u32[]{:S(2)}, u32[]{:S(2)}) collective-permute-start(f32[96,384]{1,0:T(8,128)} %slice_bitcast_fusion.3), channel_id=1, source_target_pairs={{2,0},{4,2},{6,4},{3,1},{5,3},{7,5},{10,8},{12,10},{14,12},{11,9},... | collective-permute-start | bytes 442376 | tf_op jit(solution)/shard_map/ppermute | solution.py:712
  130.4 105.0 %collective-permute-start.10 = (f32[4,96,384]{2,1,0:T(8,128)}, f32[4,96,384]{2,1,0:T(8,128)}, u32[]{:S(2)}, u32[]{:S(2)}) collective-permute-start(f32[4,96,384]{2,1,0:T(8,128)} %get-tuple-element.333), channel_id=1, source_target_pairs={{8,0},{9,1},{10,2},{11,3},{12,4},{13,5},{14,6},{15,7},{24,16},{25,... | collective-permute-start | bytes 1769480 | tf_op jit(solution)/shard_map/ppermute | solution.py:609
  131.7 4.8 %collective-permute-start.11 = (f32[96,384]{1,0:T(8,128)}, f32[96,384]{1,0:T(8,128)}, u32[]{:S(2)}, u32[]{:S(2)}) collective-permute-start(f32[96,384]{1,0:T(8,128)} %get-tuple-element.336), channel_id=1, source_target_pairs={{32,34},{38,36},{96,98},{102,100},{128,130},{134,132},{192,194},{1... | collective-permute-start | bytes 442376 | tf_op jit(solution)/shard_map/ppermute | solution.py:752
  134.6 7.9 %collective-permute-start.12 = (f32[96,384]{1,0:T(8,128)}, f32[96,384]{1,0:T(8,128)}, u32[]{:S(2)}, u32[]{:S(2)}) collective-permute-start(f32[96,384]{1,0:T(8,128)} %slice_bitcast_fusion.2), channel_id=1, source_target_pairs={{2,0},{4,2},{6,4},{3,1},{5,3},{7,5},{10,8},{12,10},{14,12},{11,9},... | collective-permute-start | bytes 442376 | tf_op jit(solution)/shard_map/ppermute | solution.py:714
  143.1 0.7 collective-permute-start.13
  143.8 1.9 collective-permute-start.14
  147.8 99.3 %all-to-all-start.5 = ((f32[256,1,16]{2,1,0:T(1,128)}), f32[256,1,16]{2,1,0:T(1,128)S(1)}, u32[]{:S(2)}, u32[]{:S(2)}) async-start(f32[256,1,16]{2,1,0:T(1,128)} %bitcast.48), calls=%async_computation.5 | async-start | bytes 262144 | tf_op jit(solution)/shard_map/all_to_all | solution.py:770
  247.0 13.1 %all-to-all-start.4 = ((f32[4,96,384]{2,1,0:T(8,128)}), f32[4,96,384]{2,1,0:T(8,128)S(1)}, u32[]{:S(2)}, u32[]{:S(2)}) async-start(f32[4,96,384]{2,1,0:T(8,128)} %broadcast_select_fusion), calls=%async_computation.4 | async-start | bytes 1179648 | tf_op jit(solution)/shard_map/all_to_all | solution.py:760
